TPU v7x, 32 devices: a 4x4x1 block of a 4x4x8 slice. The times are simulated.
32 devices in a mesh: rep: 2 (over z, core), dp: 16 (over x, y).
Axes of the slice: x: 4, y: 4, z: 1, core: 2. Of those that a mesh axis runs over, the one named last changes fastest.
The devices are a block of a 4x4x8 slice.
Arguments:
- x: bfloat16 [32, 1024, 512], P(('rep', 'dp')), parts along dimension 0
- dy: bfloat16 [32, 1024, 512], P(('rep', 'dp')), parts along dimension 0
- w_gate: bfloat16 [2, 512, 8192], P(None, 'dp')
- w_up: bfloat16 [2, 512, 8192], P(None, 'dp')
- w_down: bfloat16 [2, 8192, 512], P(None, 'dp')
- m_w_gate: float32 [2, 512, 8192], P(None, 'dp')
- m_w_up: float32 [2, 512, 8192], P(None, 'dp')
- m_w_down: float32 [2, 8192, 512], P(None, 'dp')
- v_w_gate: float32 [2, 512, 8192], P(None, 'dp')
- v_w_up: float32 [2, 512, 8192], P(None, 'dp')
- v_w_down: float32 [2, 8192, 512], P(None, 'dp')
Outputs:
- output 1: bfloat16 [4, 512, 8192], P('rep', 'dp'), parts along dimension 0
- output 2: bfloat16 [4, 512, 8192], P('rep', 'dp'), parts along dimension 0
- output 3: bfloat16 [4, 8192, 512], P('rep', 'dp'), parts along dimension 0
- output 4: float32 [4, 512, 8192], P('rep', 'dp'), parts along dimension 0
- output 5: float32 [4, 512, 8192], P('rep', 'dp'), parts along dimension 0
- output 6: float32 [4, 8192, 512], P('rep', 'dp'), parts along dimension 0
- output 7: float32 [4, 512, 8192], P('rep', 'dp'), parts along dimension 0
- output 8: float32 [4, 512, 8192], P('rep', 'dp'), parts along dimension 0
- output 9: float32 [4, 8192, 512], P('rep', 'dp'), parts along dimension 0
There are 2 independent parts. A program takes and returns all parts, laid end to end along the dimension named above; an argument that names none is the same for every part.
All inputs are finite; a program needn't handle non-finite values.
Results may differ from a plain program's by a relative error of at most 0.022.
Values are sent between devices in bfloat16 or wider.
A program may use at most 768 MiB of HBM per device.

v0:
```python
import jax
import jax.numpy as jnp
from jax import lax
from jax.sharding import PartitionSpec as P

NAMES = ("w_gate", "w_up", "w_down")


def matmul(a, w):
    return jnp.dot(a, w, preferred_element_type=jnp.float32).astype(jnp.bfloat16)


def normed(h):
    wide = h.astype(jnp.float32)
    scale = lax.rsqrt(jnp.mean(wide**2, -1, keepdims=True) + 1e-6)
    return (wide * scale).astype(jnp.bfloat16)


def layer(h, w):
    a = normed(h)
    gate = jnp.dot(a, w["w_gate"], preferred_element_type=jnp.float32)
    up = jnp.dot(a, w["w_up"], preferred_element_type=jnp.float32)
    return h + matmul((jax.nn.silu(gate) * up).astype(jnp.bfloat16), w["w_down"])


def adamw(w, m, v, g):
    m = 0.9 * m + 0.1 * g
    v = 0.95 * v + 0.05 * g * g
    step = m * lax.rsqrt(v + 1e-8) + 0.1 * w
    return (w - 0.02 * step).astype(jnp.bfloat16), m, v


def solution(mesh):
    def fetched(weights, number):
        return {name: lax.all_gather(w[number], "dp", axis=0, tiled=True) for name, w in zip(NAMES, weights, strict=True)}

    def step(x, dy, *arrays):
        weights, m, v = (arrays[i : i + 3] for i in (0, 3, 6))
        layers = weights[0].shape[0]
        h, kept = x[0], []
        for number in range(layers):
            kept.append(h)
            h = layer(h, fetched(weights, number))
        by_h, mine = dy[0], [None] * layers
        for number in reversed(range(layers)):
            _, back = jax.vjp(lambda w, h: layer(h, w), fetched(weights, number), kept[number])
            by_w, by_h = back(by_h)
            mine[number] = [lax.psum_scatter(by_w[name], "dp", scatter_dimension=0, tiled=True) for name in NAMES]
        gradients = [jnp.stack([mine[number][i] for number in range(layers)]).astype(jnp.float32) for i in range(3)]
        new = [adamw(w.astype(jnp.float32), m, v, g) for w, m, v, g in zip(weights, m, v, gradients, strict=True)]
        return tuple(one[which] for which in range(3) for one in new)

    states, cut = P(("rep", "dp"), None, None), P(None, "dp", None)
    return jax.shard_map(
        step,
        mesh=mesh,
        in_specs=(states, states) + (cut,) * 9,
        out_specs=(P("rep", "dp", None),) * 9,
        check_vma=False,
    )
```

profile of v0, /device:TPU:97, one launch (start us, length us, event | category | flops | bytes accessed | tf_op | source)
XLA Modules:
  0.0 1015.6 jit_solution(16130074831421099094)
XLA Ops:
  7.3 2.4 fusion.99
  9.8 2.2 fusion.98
  12.2 2.2 fusion.97
  18.6 61.1 %all-gather.13.cloned.1.call-done = bf16[1,512,8192]{2,1,0:T(8,128)(2,1)} async-done(((bf16[1,32,8192]{2,1,0:T(8,128)(2,1)}), bf16[1,512,8192]{2,1,0:T(8,128)(2,1)}) %all-gather.13.cloned.1.call-update) | async-done | bytes 8388624 | tf_op jit(solution)/shard_map/all_gather | solution.py:35
  79.7 18.7 %fusion.34 = f32[1024,8192]{1,0:T(8,128)} fusion(bf16[1,512,8192]{2,1,0:T(8,128)(2,1)} %all-gather.13.cloned.1.call-done, bf16[1,1024,512]{1,2,0:T(8,128)(2,1)S(1)} %copy.20, f32[1024]{0:T(1024)S(1)} %add_rsqrt_fusion), kind=kOutput, calls=%fused_computation.45 | convolution fusion | flops 8591507456 | bytes 42995712 | tf_op jit(solution)/shard_map/dot_general | solution.py:21
  98.4 49.0 %all-gather.15.cloned.1.call-done = bf16[1,512,8192]{2,1,0:T(8,128)(2,1)} async-done(((bf16[1,32,8192]{2,1,0:T(8,128)(2,1)}), bf16[1,512,8192]{2,1,0:T(8,128)(2,1)}) %all-gather.15.cloned.1.call-update) | async-done | bytes 8388624 | tf_op jit(solution)/shard_map/all_gather | solution.py:35
  147.4 33.2 %multiply_convert_fusion.1 = (bf16[1024,8192]{1,0:T(8,128)(2,1)}, f32[1024,8192]{1,0:T(8,128)}) fusion(f32[1024,8192]{1,0:T(8,128)} %fusion.34, bf16[1,512,8192]{2,1,0:T(8,128)(2,1)} %all-gather.15.cloned.1.call-done, bf16[1,1024,512]{1,2,0:T(8,128)(2,1)S(1)} %copy.20, f32[1024]{0:T(1024)S(1)} %add_rsqrt_fusion), kind=kOutput, calls=%fused_computation.17 | convolution fusion | flops 8641839104 | bytes 93327360 | tf_op jit(solution)/shard_map/dot_general | solution.py:22
  180.6 34.5 %all-gather.17.cloned.1.call-done = bf16[1,8192,512]{2,1,0:T(8,128)(2,1)} async-done(((bf16[1,512,512]{2,1,0:T(8,128)(2,1)}), bf16[1,8192,512]{2,1,0:T(8,128)(2,1)}) %all-gather.17.cloned.1.call-update) | async-done | bytes 8388624 | tf_op jit(solution)/shard_map/all_gather | solution.py:35
  215.1 15.1 %fusion.56 = (f32[1024]{0:T(1024)S(1)}, bf16[1024,512]{0,1:T(8,128)(2,1)S(1)}) fusion(bf16[1024,8192]{1,0:T(8,128)(2,1)} %get-tuple-element.24, bf16[1,8192,512]{2,1,0:T(8,128)(2,1)} %all-gather.17.cloned.1.call-done, bf16[1,1024,512]{1,2,0:T(8,128)(2,1)S(1)} %copy.20), kind=kOutput, calls=%fused_computation.85 | convolution fusion | flops 8592555008 | bytes 27267072 | tf_op jit(solution)/shard_map/dot_general | solution.py:10
  230.3 52.3 %all-gather.21.cloned.1.call-done = bf16[1,8192,512]{2,1,0:T(8,128)(2,1)} async-done(((bf16[1,512,512]{2,1,0:T(8,128)(2,1)}), bf16[1,8192,512]{2,1,0:T(8,128)(2,1)}) %all-gather.21.cloned.1.call-update) | async-done | bytes 8388624 | tf_op jit(solution)/shard_map/all_gather | solution.py:35
  282.6 15.1 %convolution_convert_fusion.1 = bf16[1024,8192]{1,0:T(8,128)(2,1)} fusion(bf16[1,8192,512]{2,1,0:T(8,128)(2,1)} %all-gather.21.cloned.1.call-done, bf16[1,1024,512]{2,1,0:T(8,128)(2,1)S(1)} %copy-done.9), kind=kOutput, calls=%fused_computation.25 | convolution fusion | flops 8598323200 | bytes 26214400 | tf_op jit(solution)/shard_map/transpose(jvp())/dot_general | solution.py:10
  297.7 52.4 %all-gather.23.cloned.1.call-done = bf16[1,512,8192]{2,1,0:T(8,128)(2,1)} async-done(((bf16[1,32,8192]{2,1,0:T(8,128)(2,1)}), bf16[1,512,8192]{2,1,0:T(8,128)(2,1)}) %all-gather.23.cloned.1.call-update) | async-done | bytes 8388624 | tf_op jit(solution)/shard_map/all_gather | solution.py:35
  350.1 18.7 %fusion.21 = f32[1024,8192]{1,0:T(8,128)} fusion(bf16[1,512,8192]{2,1,0:T(8,128)(2,1)} %all-gather.23.cloned.1.call-done, bf16[1024,512]{0,1:T(8,128)(2,1)S(1)} %get-tuple-element.27, f32[1024]{0:T(1024)S(1)} %fusion.85), kind=kOutput, calls=%fused_computation.32 | convolution fusion | flops 8591507456 | bytes 42995712 | tf_op jit(solution)/shard_map/jvp()/dot_general | solution.py:22
  368.8 48.8 %all-gather.19.cloned.1.call-done = bf16[1,512,8192]{2,1,0:T(8,128)(2,1)} async-done(((bf16[1,32,8192]{2,1,0:T(8,128)(2,1)}), bf16[1,512,8192]{2,1,0:T(8,128)(2,1)}) %all-gather.19.cloned.1.call-update) | async-done | bytes 8388624 | tf_op jit(solution)/shard_map/all_gather | solution.py:35
  417.6 41.1 %fusion.2 = (bf16[1024,8192]{1,0:T(8,128)(2,1)}, f32[1024,8192]{1,0:T(8,128)}) fusion(f32[1024,8192]{1,0:T(8,128)} %fusion.21, bf16[1024,8192]{1,0:T(8,128)(2,1)} %convolution_convert_fusion.1, bf16[1,512,8192]{2,1,0:T(8,128)(2,1)} %all-gather.19.cloned.1.call-done, bf16[1024,512]{0,1:T(8,128)(2,1)S(1)} %get-tuple-element.27, f32[1024]{0:T(1024)S(1)} %fusion.85), kind=kOutput, calls=%fused_computation.8 | convolution fusion | flops 8692170752 | bytes 110104576 | tf_op jit(solution)/shard_map/jvp()/dot_general | solution.py:21
  458.7 21.1 %fusion.65 = bf16[1024,512]{0,1:T(8,128)(2,1)S(1)} fusion(bf16[1,512,8192]{2,1,0:T(8,128)(2,1)} %all-gather.23.cloned.1.call-done, bf16[1024,8192]{1,0:T(8,128)(2,1)} %convolution_convert_fusion.1, f32[1024,8192]{1,0:T(8,128)} %get-tuple-element.29), kind=kOutput, calls=%fused_computation.90 | convolution fusion | flops 8640790528 | bytes 59768832 | tf_op jit(solution)/shard_map/transpose(jvp())/dot_general | solution.py:22
  479.9 12.8 %fusion.58 = (f32[1024]{0:T(1024)S(1)}, bf16[1024,512]{0,1:T(8,128)(2,1)S(1)}) fusion(bf16[1024,512]{0,1:T(8,128)(2,1)S(1)} %get-tuple-element.27, bf16[1024,512]{0,1:T(8,128)(2,1)S(1)} %fusion.65, bf16[1024,8192]{1,0:T(8,128)(2,1)} %get-tuple-element.28, bf16[1,512,8192]{2,1,0:T(8,128)(2,1)S(1)} %copy-done.17), kind=kOutput, calls=%fused_computation.87 | convolution fusion | flops 8592555008 | bytes 28315648 | tf_op jit(solution)/shard_map/transpose(jvp())/dot_general | solution.py:21
  493.5 17.4 %convolution_convert_fusion.2 = bf16[8192,512]{1,0:T(8,128)(2,1)} fusion(bf16[1024,8192]{1,0:T(8,128)(2,1)} %get-tuple-element.24, bf16[1024,512]{0,1:T(8,128)(2,1)S(1)} %fusion.74), kind=kOutput, calls=%fused_computation.30 | convolution fusion | flops 8594128896 | bytes 26214400 | tf_op jit(solution)/shard_map/transpose(jvp())/dot_general | solution.py:10
  512.1 26.8 %fusion.18 = bf16[8192,512]{1,0:T(8,128)(2,1)} fusion(f32[1024,8192]{1,0:T(8,128)} %fusion.21, bf16[1,1024,512]{2,1,0:T(8,128)(2,1)S(1)} %copy-done.10, f32[1024,8192]{1,0:T(8,128)} %get-tuple-element.29), kind=kOutput, calls=%fused_computation.27 | convolution fusion | flops 8644460544 | bytes 76546048 | tf_op jit(solution)/shard_map/transpose(jvp())/dot_general | solution.py:10
  539.1 16.1 %convolution_convert_fusion = bf16[1024,8192]{1,0:T(8,128)(2,1)} fusion(bf16[1024,512]{0,1:T(8,128)(2,1)S(1)} %fusion.74, bf16[1,8192,512]{2,1,0:T(8,128)(2,1)} %all-gather.17.cloned.1.call-done), kind=kOutput, calls=%fused_computation.24 | convolution fusion | flops 8598323200 | bytes 26214400 | tf_op jit(solution)/shard_map/transpose(jvp())/dot_general | solution.py:10
  555.1 22.2 %fusion.20 = bf16[512,8192]{1,0:T(8,128)(2,1)} fusion(bf16[1024,8192]{1,0:T(8,128)(2,1)} %convolution_convert_fusion, f32[1024,8192]{1,0:T(8,128)} %fusion.34, bf16[1,1024,512]{1,2,0:T(8,128)(2,1)S(1)} %copy-done.1, f32[1024]{0:T(1024)S(1)} %copy-done.14), kind=kOutput, calls=%fused_computation.29 | convolution fusion | flops 8646033408 | bytes 59772928 | tf_op jit(solution)/shard_map/transpose(jvp())/dot_general | solution.py:22
  578.6 22.4 %fusion.19 = bf16[512,8192]{1,0:T(8,128)(2,1)} fusion(bf16[1024,8192]{1,0:T(8,128)(2,1)} %convolution_convert_fusion.1, bf16[1024,512]{0,1:T(8,128)(2,1)S(1)} %copy-done.3, f32[1024]{0:T(1024)S(1)} %copy-done.12, f32[1024,8192]{1,0:T(8,128)} %get-tuple-element.29), kind=kOutput, calls=%fused_computation.28 | convolution fusion | flops 8646033408 | bytes 59772928 | tf_op jit(solution)/shard_map/transpose(jvp())/dot_general | solution.py:22
  601.1 32.9 %fusion.15 = bf16[512,8192]{1,0:T(8,128)(2,1)} fusion(f32[1024,8192]{1,0:T(8,128)} %fusion.34, f32[1024,8192]{1,0:T(8,128)} %get-tuple-element.25, bf16[1024,8192]{1,0:T(8,128)(2,1)} %convolution_convert_fusion, bf16[1,1024,512]{1,2,0:T(8,128)(2,1)S(1)} %copy-done.1, f32[1024]{0:T(1024)S(1)} %copy-done.14), kind=kOutput, calls=%fused_computation.26 | convolution fusion | flops 8687976448 | bytes 93327360 | tf_op jit(solution)/shard_map/transpose(jvp())/dot_general | solution.py:21
  634.2 17.1 %convolution_convert_fusion.3 = bf16[512,8192]{1,0:T(8,128)(2,1)} fusion(bf16[1024,8192]{1,0:T(8,128)(2,1)} %get-tuple-element.28, bf16[1024,512]{0,1:T(8,128)(2,1)S(1)} %copy-done.3, f32[1024]{0:T(1024)S(1)} %copy-done.12), kind=kOutput, calls=%fused_computation.31 | convolution fusion | flops 8591507456 | bytes 26218496 | tf_op jit(solution)/shard_map/transpose(jvp())/dot_general | solution.py:21
  651.4 20.9 %reduce-scatter.17.cloned.1.call-done = bf16[512,512]{1,0:T(8,128)(2,1)} async-done(((bf16[8192,512]{1,0:T(8,128)(2,1)}), bf16[512,512]{1,0:T(8,128)(2,1)}) %reduce-scatter.17.cloned.1.call-update) | async-done | bytes 524304 | tf_op jit(solution)/shard_map/reduce_scatter | solution.py:48
  672.3 5.6 fusion.51
  677.9 77.1 %reduce-scatter.11.cloned.1.call-done = bf16[32,8192]{1,0:T(8,128)(2,1)} async-done(((bf16[512,8192]{1,0:T(8,128)(2,1)}), bf16[32,8192]{1,0:T(8,128)(2,1)}) %reduce-scatter.11.cloned.1.call-update) | async-done | bytes 524304 | tf_op jit(solution)/shard_map/reduce_scatter | solution.py:48
  755.0 82.4 %reduce-scatter.13.cloned.1.call-done = bf16[32,8192]{1,0:T(8,128)(2,1)} async-done(((bf16[512,8192]{1,0:T(8,128)(2,1)}), bf16[32,8192]{1,0:T(8,128)(2,1)}) %reduce-scatter.13.cloned.1.call-update) | async-done | bytes 524304 | tf_op jit(solution)/shard_map/reduce_scatter | solution.py:48
  837.4 5.4 fusion.47
  842.9 77.3 %reduce-scatter.7.cloned.1.call-done = bf16[32,8192]{1,0:T(8,128)(2,1)} async-done(((bf16[512,8192]{1,0:T(8,128)(2,1)}), bf16[32,8192]{1,0:T(8,128)(2,1)}) %reduce-scatter.7.cloned.1.call-update) | async-done | bytes 524304 | tf_op jit(solution)/shard_map/reduce_scatter | solution.py:48
  920.1 82.6 %reduce-scatter.9.cloned.1.call-done = bf16[32,8192]{1,0:T(8,128)(2,1)} async-done(((bf16[512,8192]{1,0:T(8,128)(2,1)}), bf16[32,8192]{1,0:T(8,128)(2,1)}) %reduce-scatter.9.cloned.1.call-update) | async-done | bytes 524304 | tf_op jit(solution)/shard_map/reduce_scatter | solution.py:48
  1002.8 5.4 fusion.39
  (68 shorter events, 8.1 us)
Async XLA Ops:
  7.2 9.3 copy-start.8
  7.2 10.1 copy-start.9
  7.2 72.5 %all-gather.13.cloned.1.call-start = ((), (), s32[]{:S(2)}) async-start(), calls=%async_computation.12 | async-start | bytes 8912896 | tf_op jit(solution)/shard_map/all_gather | solution.py:35
  9.7 137.7 %all-gather.15.cloned.1.call-start = ((), (), s32[]{:S(2)}) async-start(), calls=%async_computation.13 | async-start | bytes 8912896 | tf_op jit(solution)/shard_map/all_gather | solution.py:35
  12.1 203.0 %all-gather.17.cloned.1.call-start = ((), (), s32[]{:S(2)}) async-start(), calls=%async_computation.14 | async-start | bytes 8912896 | tf_op jit(solution)/shard_map/all_gather | solution.py:35
  14.4 268.1 %all-gather.21.cloned.1.call-start = ((), (), s32[]{:S(2)}) async-start(), calls=%async_computation.16 | async-start | bytes 8912896 | tf_op jit(solution)/shard_map/all_gather | solution.py:35
  15.1 335.0 %all-gather.23.cloned.1.call-start = ((), (), s32[]{:S(2)}) async-start(), calls=%async_computation.17 | async-start | bytes 8912896 | tf_op jit(solution)/shard_map/all_gather | solution.py:35
  15.7 401.9 %all-gather.19.cloned.1.call-start = ((), (), s32[]{:S(2)}) async-start(), calls=%async_computation.15 | async-start | bytes 8912896 | tf_op jit(solution)/shard_map/all_gather | solution.py:35
  16.4 635.0 %reduce-scatter.15.cloned.1.call-start = ((), (), s32[]{:S(2)}) async-start(), calls=%async_computation.10 | async-start | bytes 8912896 | tf_op jit(solution)/shard_map/reduce_scatter | solution.py:48
  17.0 198.1 %copy-start = (bf16[1,1024,512]{1,2,0:T(8,128)(2,1)}, bf16[1,1024,512]{1,2,0:T(8,128)(2,1)S(1)}, u32[]{:S(2)}) copy-start(bf16[1,1024,512]{1,2,0:T(8,128)(2,1)S(1)} %copy.20) | copy-start | bytes 3145732
  17.3 130.1 %copy-start.13 = (f32[1024]{0:T(1024)}, f32[1024]{0:T(1024)S(1)}, u32[]{:S(2)}) copy-start(f32[1024]{0:T(1024)S(1)} %add_rsqrt_fusion) | copy-start | bytes 12292
  230.2 67.5 %copy-start.15 = (f32[1024]{0:T(1024)}, f32[1024]{0:T(1024)S(1)}, u32[]{:S(2)}) copy-start(f32[1024]{0:T(1024)S(1)} %get-tuple-element.26) | copy-start | bytes 12292
  230.2 262.6 %copy-start.2 = (bf16[1024,512]{0,1:T(8,128)(2,1)}, bf16[1024,512]{0,1:T(8,128)(2,1)S(1)}, u32[]{:S(2)}) copy-start(bf16[1024,512]{0,1:T(8,128)(2,1)S(1)} %get-tuple-element.27) | copy-start | bytes 3145732
  230.3 262.5 %copy-start.11 = (f32[1024]{0:T(1024)}, f32[1024]{0:T(1024)S(1)}, u32[]{:S(2)}) copy-start(f32[1024]{0:T(1024)S(1)} %fusion.85) | copy-start | bytes 12292
  458.7 21.1 %copy-start.17 = (bf16[1,512,8192]{2,1,0:T(8,128)(2,1)S(1)}, bf16[1,512,8192]{2,1,0:T(8,128)(2,1)}, u32[]{:S(2)}) copy-start(bf16[1,512,8192]{2,1,0:T(8,128)(2,1)} %all-gather.19.cloned.1.call-done) | copy-start | bytes 25165828
  479.9 12.9 %copy-start.16 = (f32[1024]{0:T(1024)S(1)}, f32[1024]{0:T(1024)}, u32[]{:S(2)}) copy-start(f32[1024]{0:T(1024)} %copy-done.15) | copy-start | bytes 12292
  479.9 12.9 %copy-start.4 = (bf16[1,1024,512]{1,2,0:T(8,128)(2,1)S(1)}, bf16[1,1024,512]{1,2,0:T(8,128)(2,1)}, u32[]{:S(2)}) copy-start(bf16[1,1024,512]{1,2,0:T(8,128)(2,1)} %copy.21) | copy-start | bytes 3145732
  510.9 1.2 copy-start.10
  511.0 161.3 %reduce-scatter.17.cloned.1.call-start = ((), (), s32[]{:S(2)}) async-start(), calls=%async_computation.11 | async-start | bytes 8912896 | tf_op jit(solution)/shard_map/reduce_scatter | solution.py:48
  539.0 16.2 %copy-start.1 = (bf16[1,1024,512]{1,2,0:T(8,128)(2,1)S(1)}, bf16[1,1024,512]{1,2,0:T(8,128)(2,1)}, u32[]{:S(2)}) copy-start(bf16[1,1024,512]{1,2,0:T(8,128)(2,1)} %copy-done) | copy-start | bytes 3145732
  539.0 16.1 %copy-start.14 = (f32[1024]{0:T(1024)S(1)}, f32[1024]{0:T(1024)}, u32[]{:S(2)}) copy-start(f32[1024]{0:T(1024)} %copy-done.13) | copy-start | bytes 12292
  539.0 216.0 %reduce-scatter.11.cloned.1.call-start = ((), (), s32[]{:S(2)}) async-start(), calls=%async_computation.8 | async-start | bytes 8912896 | tf_op jit(solution)/shard_map/reduce_scatter | solution.py:48
  577.3 1.2 copy-start.3
  577.3 1.2 copy-start.12
  577.4 260.0 %reduce-scatter.13.cloned.1.call-start = ((), (), s32[]{:S(2)}) async-start(), calls=%async_computation.9 | async-start | bytes 8912896 | tf_op jit(solution)/shard_map/reduce_scatter | solution.py:48
  601.1 319.1 %reduce-scatter.7.cloned.1.call-start = ((), (), s32[]{:S(2)}) async-start(), calls=%async_computation.6 | async-start | bytes 8912896 | tf_op jit(solution)/shard_map/reduce_scatter | solution.py:48
  634.1 368.7 %reduce-scatter.9.cloned.1.call-start = ((), (), s32[]{:S(2)}) async-start(), calls=%async_computation.7 | async-start | bytes 8912896 | tf_op jit(solution)/shard_map/reduce_scatter | solution.py:48
  651.3 21.0 %copy-start.5 = (bf16[2,512,512]{2,1,0:T(8,128)(2,1)S(1)}, bf16[2,512,512]{2,1,0:T(8,128)(2,1)}, u32[]{:S(2)}) copy-start(bf16[2,512,512]{2,1,0:T(8,128)(2,1)} %param.15) | copy-start | bytes 3145732
  651.3 186.2 %copy-start.6 = (bf16[2,32,8192]{2,1,0:T(8,128)(2,1)S(1)}, bf16[2,32,8192]{2,1,0:T(8,128)(2,1)}, u32[]{:S(2)}) copy-start(bf16[2,32,8192]{2,1,0:T(8,128)(2,1)} %param.14) | copy-start | bytes 3145732
  677.9 324.8 %copy-start.7 = (bf16[2,32,8192]{2,1,0:T(8,128)(2,1)S(1)}, bf16[2,32,8192]{2,1,0:T(8,128)(2,1)}, u32[]{:S(2)}) copy-start(bf16[2,32,8192]{2,1,0:T(8,128)(2,1)} %param.13) | copy-start | bytes 3145732
Sparse Core Ops, SparseCore 0:
  10.6 69.1 all-gather.12
  82.2 65.0 all-gather.14
  149.9 65.0 all-gather.16
  217.5 65.0 all-gather.20
  285.0 65.0 all-gather.22
  352.5 65.1 all-gather.18
  511.1 78.3 reduce-scatter.14
  592.8 79.4 reduce-scatter.16
  675.5 79.4 reduce-scatter.10
  758.1 79.2 reduce-scatter.12
  840.7 79.4 reduce-scatter.6
  923.2 79.4 reduce-scatter.8
where the time goes:
time: 1020 us
  waiting for transfers between devices  641 us (63%)
  matrix products  331 us (32%)
  other arithmetic  17.5 us (2%)
  between operations  15 us (1%)
  local copies, waits for them, and re-layouts  11 us (1%)
    reduce_scatter x6, waiting for transfers between devices, step(): lax.psum_scatter(by_w[name], 'dp', scatter_dimension=0, tiled=True)  340 us
    all_gather x6, waiting for transfers between devices, fetched(): lax.all_gather(w[number], 'dp', axis=0, tiled=True)  298 us
    dot_general x5, matrix products, layer(): gate = jnp.dot(a, w['w_gate'], preferred_element_type=jnp.float32)  123 us
    dot_general x5, matrix products, layer(): up = jnp.dot(a, w['w_up'], preferred_element_type=jnp.float32)  118 us
    dot_general x5, matrix products, matmul(): jnp.dot(a, w, preferred_element_type=jnp.float32).astype(jnp.bfloat16)  90.5 us
  transfers between devices with their start and end apart: 12, of which 11 were waited for; matrix products, arithmetic and copies ran while one was open for 25% of the time, Pallas kernels for 0%

commit v1 on v0

v1 whole, which is shorter than its diff:
```python
import math

import jax
import jax.numpy as jnp
from jax import lax
from jax.experimental import pallas as pl
from jax.experimental.pallas import tpu as pltpu
from jax.sharding import PartitionSpec as P

MESH = pl.DeviceIdType.MESH
BF16, F32 = jnp.bfloat16, jnp.float32
TILE = 512
SUB = 512
SLOTS = 3


def adamw(w, m, v, g):
    m = 0.9 * m + 0.1 * g
    v = 0.95 * v + 0.05 * g * g
    step = m * lax.rsqrt(v + 1e-8) + 0.1 * w
    return (w - 0.02 * step).astype(BF16), m, v


def nn(a, b):
    return lax.dot_general(a, b, (((1,), (0,)), ((), ())), preferred_element_type=F32)


def nt(a, b):
    return lax.dot_general(a, b, (((1,), (1,)), ((), ())), preferred_element_type=F32)


def scale_of(wide):
    return lax.rsqrt(jnp.mean(wide * wide, -1, keepdims=True) + 1e-6)


def make_kernel(n, tokens, dim, rows, wide_cols, deep, layers):
    total = 2 * tokens
    hidden = wide_cols // 2
    chunk = hidden // n
    subs = chunk // SUB
    tiles = total // TILE
    tiles_seq = tokens // TILE
    per_sub = SUB // deep
    last = layers * n

    def kernel(
        x_ref, dy_ref, wg_ref, wu_ref, wd_ref, pgu, pd,
        GU, D, RG, RD, xb, dyb, a0, a1, aT, dT, pacc, precv, actb, dgb, dub, SGU, SD,
        ld_sem, q_loc, q_send, q_recv, ag_send, ag_recv, ex_send, ex_recv, y_send, y_recv, credit, x_send, p_recv, pd_recv,
    ):
        rep, dp = lax.axis_index("rep"), lax.axis_index("dp")
        c, base = rep % 2, (rep // 2) * 2
        x, y = dp // n, dp % n
        role = x % 2
        sib = (base + 1 - c, dp)

        def at(px, py, core=None):
            return (base + (c if core is None else core), px * n + py)

        def hop(axis, sign):
            return at((x + sign) % n, y) if axis == 0 else at(x, (y + sign) % n)

        for l in range(layers):

            @pl.loop(0, n * n)
            def _(d, l=l):
                for m, w in enumerate((wg_ref, wu_ref)):
                    pltpu.make_async_copy(
                        w.at[l, :, pl.ds(pl.multiple_of(d * 2 * deep + c * deep, deep), deep)],
                        GU.at[l, x, y, :, pl.ds(pl.multiple_of((d // n) * 2 * chunk + m * chunk + (d % n) * deep, deep), deep)],
                        ld_sem.at[l, 0],
                    ).start()

            pltpu.make_async_copy(wd_ref.at[l, pl.ds(pl.multiple_of(c * deep, deep), deep), :], D.at[l, x, y], ld_sem.at[l, 1]).start()

        def own_loaded(l):
            pltpu.make_async_copy(GU.at[l, x, y], GU.at[l, x, y], ld_sem.at[l, 0]).wait()
            pltpu.make_async_copy(D.at[l, x, y], D.at[l, x, y], ld_sem.at[l, 1]).wait()

        barrier = pltpu.get_barrier_semaphore()
        friends = [sib, hop(1, 1), hop(1, -1)]
        for o in range(1, n):
            for core in range(2):
                friends.append(at((x + o) % n, y, core))
        for f in friends:
            pl.semaphore_signal(barrier, inc=1, device_id=f, device_id_type=MESH)
        pl.semaphore_wait(barrier, len(friends))

        def remote(src, dst, ss, rs, dev):
            return pltpu.make_async_remote_copy(src_ref=src, dst_ref=dst, send_sem=ss, recv_sem=rs, device_id=dev, device_id_type=MESH)

        def piece(b, l, path, p, q, half):
            px, py = (p, q) if path == 0 else (q, p)
            if b == 0:
                r, h = rows // 2, wide_cols // 2
                cols = slice(None) if half is None else pl.ds(half * h, h)
                return GU.at[l, px, py, pl.ds(path * r, r), cols]
            r = deep // 2
            if half is None:
                return D.at[l, px, py, pl.ds(path * r, r), :]
            return D.at[l, px, py, pl.ds(path * r + half * (r // 2), r // 2), :]

        def moved(l, path, p, q, half, axis, sign, cls, ev):
            dev = hop(axis if path == 0 else 1 - axis, sign)
            return [
                remote(piece(b, l, path, p, q, half), piece(b, l, path, p, q, half), ag_send.at[l, cls, b], ag_recv.at[l, path, ev, b], dev)
                for b in range(2)
            ]

        def send(*args):
            for one in moved(*args):
                one.start()

        def arrived(l, path, p, q, half, ev):
            for one in moved(l, path, p, q, half, 0, 1, 0, ev):
                one.wait_recv()

        paths = ((0, x, y), (1, y, x))

        def gather(l, stage):
            for path, p, q in paths:
                pm, pp, p2, qm, qp = (p + n - 1) % n, (p + 1) % n, (p + 2) % n, (q + n - 1) % n, (q + 1) % n
                if stage == 0:
                    send(l, path, p, q, None, 0, 1, 0, 0)
                    send(l, path, p, q, None, 0, -1, 0, 1)
                    send(l, path, p, q, None, 1, 1, 0, 4)
                    send(l, path, p, q, None, 1, -1, 0, 9)
                if stage == 1:
                    arrived(l, path, pm, q, None, 0)
                    send(l, path, pm, q, 0, 0, 1, 2, 2)
                    send(l, path, pm, q, None, 1, 1, 0, 5)
                    send(l, path, pm, q, None, 1, -1, 0, 10)
                    arrived(l, path, pp, q, None, 1)
                    send(l, path, pp, q, 1, 0, -1, 2, 3)
                    send(l, path, pp, q, None, 1, 1, 0, 6)
                    send(l, path, pp, q, None, 1, -1, 0, 11)
                if stage == 2:
                    arrived(l, path, p, qm, None, 4)
                    send(l, path, p, qm, 0, 1, 1, 3, 14)
                    arrived(l, path, p, qp, None, 9)
                    send(l, path, p, qp, 1, 1, -1, 3, 14)
                    arrived(l, path, p2, q, 0, 2)
                    send(l, path, p2, q, 0, 1, 1, 1, 7)
                    send(l, path, p2, q, 0, 1, -1, 1, 12)
                    arrived(l, path, p2, q, 1, 3)
                    send(l, path, p2, q, 1, 1, 1, 1, 8)
                    send(l, path, p2, q, 1, 1, -1, 1, 13)
                if stage == 3:
                    arrived(l, path, pm, qm, None, 5)
                    send(l, path, pm, qm, 0, 1, 1, 3, 14)
                    arrived(l, path, pm, qp, None, 10)
                    send(l, path, pm, qp, 1, 1, -1, 3, 14)
                    arrived(l, path, pp, qm, None, 6)
                    send(l, path, pp, qm, 0, 1, 1, 3, 14)
                    arrived(l, path, pp, qp, None, 11)
                    send(l, path, pp, qp, 1, 1, -1, 3, 14)
                if stage == 4:
                    arrived(l, path, p2, qm, 0, 7)
                    send(l, path, p2, qm, 0, 1, 1, 3, 14)
                    arrived(l, path, p2, qp, 1, 13)
                    send(l, path, p2, qp, 1, 1, -1, 3, 14)
                    arrived(l, path, p2, qm, 1, 8)
                    arrived(l, path, p2, qp, 0, 12)
                if stage == 5:
                    for b, W in enumerate((GU, D)):
                        part = W.at[l, 0, pl.ds(0, 2)]
                        remote(part, part, ag_send.at[l, 0, b], ag_recv.at[l, path, 14, b], sib).wait_recv()
            if stage == 5:
                for b, W in enumerate((GU, D)):
                    for cls, part in enumerate((W.at[l, pl.ds(0, 2)], W.at[l, 0, pl.ds(0, 2)], W.at[l, 0, 0], W.at[l, 0])):
                        remote(part, part, ag_send.at[l, cls, b], ag_recv.at[l, 0, 0, b], sib).wait_send()

        primary = c == role
        inputs = ((x_ref, xb), (dy_ref, dyb))

        def to_pair(w):
            src, buf = inputs[w]
            return remote(src.at[0], buf.at[role], q_send.at[w, 0], q_recv.at[w, 1], at(x + 1 - 2 * role, y))

        def to_sib(w, which):
            buf = inputs[w][1]
            slot = role if which == 0 else 1 - role
            return remote(buf.at[slot], buf.at[slot], q_send.at[w, which], q_recv.at[w, which], sib)

        def local(w):
            src, buf = inputs[w]
            return pltpu.make_async_copy(src.at[0], buf.at[role], q_loc.at[w])

        @pl.when(primary)
        def _():
            local(0).start()
            local(1).start()

        own_loaded(0)
        gather(0, 0)

        @pl.when(jnp.logical_not(primary))
        def _():
            to_pair(0).start()

        @pl.when(primary)
        def _():
            for w in range(2):
                local(w).wait()
                to_sib(w, 0).start()

        gather(0, 1)
        gather(0, 2)

        @pl.when(primary)
        def _():
            to_sib(0, 1).wait_recv()
            to_sib(0, 1).start()

        gather(0, 3)
        gather(0, 4)
        own_loaded(1)
        gather(1, 0)

        @pl.when(jnp.logical_not(primary))
        def _():
            to_pair(1).start()
            for which in range(2):
                to_sib(0, which).wait_recv()

        @pl.when(primary)
        def _():
            to_sib(0, 0).wait_send()
            to_sib(0, 1).wait_send()

        def norm(h, a):
            @pl.loop(0, tiles)
            def _(t):
                s, r = t // tiles_seq, pl.ds(pl.multiple_of((t % tiles_seq) * TILE, TILE), TILE)
                wide = h[s, r, :].astype(F32)
                a[pl.ds(pl.multiple_of(t * TILE, TILE), TILE), :] = (wide * scale_of(wide)).astype(BF16)

        def turned(src, dst):
            @pl.loop(0, tiles)
            def _(t):
                dst[:, pl.ds(pl.multiple_of(t * TILE, TILE), TILE)] = src(t).astype(F32).T.astype(BF16)

        def span(t):
            return pl.ds(pl.multiple_of(t * TILE, TILE), TILE)

        def seq_tile(b, t):
            return b[t // tiles_seq, pl.ds(pl.multiple_of((t % tiles_seq) * TILE, TILE), TILE), :]

        norm(xb, a0)

        def clear():
            @pl.loop(0, tiles)
            def _(t):
                pacc[span(t), :] = jnp.zeros((TILE, dim), F32)

        clear()
        gather(0, 5)

        def w_gate(l, j, i):
            return GU.at[l, :, :, :, pl.ds(pl.multiple_of(j * 2 * chunk + i * SUB, SUB), SUB)]

        def w_up(l, j, i):
            return GU.at[l, :, :, :, pl.ds(pl.multiple_of(j * 2 * chunk + chunk + i * SUB, SUB), SUB)]

        def w_down(l, j, i):
            return D.at[l, j, pl.ds(i * per_sub, per_sub), :, :]

        def flat(ref):
            v = ref[...]
            return v.reshape(math.prod(v.shape[:-1]), v.shape[-1])

        def swap_partial():
            part = pacc.at[pl.ds(pl.multiple_of((1 - c) * tokens, tokens), tokens), :]
            return remote(part, precv, ex_send.at[0], ex_recv.at[0], sib)

        def swap_state(buf, which):
            return remote(buf.at[c], buf.at[c], ex_send.at[which], ex_recv.at[which], sib)

        @pl.loop(0, tiles)
        def _(t0):
            t = (t0 + (1 - c) * tiles_seq) % tiles

            @pl.loop(0, n * subs)
            def _(f):
                j, i = f // subs, f % subs
                a = a0[span(t), :]
                gate = nn(a, flat(w_gate(0, j, i)))
                up = nn(a, flat(w_up(0, j, i)))
                act = (gate * jax.nn.sigmoid(gate) * up).astype(BF16)
                pacc[span(t), :] += nn(act, flat(w_down(0, j, i)))

            @pl.when(t0 == tiles_seq - 1)
            def _():
                swap_partial().start()

            for stage in range(1, 5):

                @pl.when(t0 == (stage - 1) * tiles // 4)
                def _(stage=stage):
                    gather(1, stage)

        @pl.when(primary)
        def _():
            to_sib(1, 1).wait_recv()
            to_sib(1, 1).start()

        swap_partial().wait()

        @pl.loop(0, tiles_seq)
        def _(t):
            mine = pl.ds(pl.multiple_of(c * tokens + t * TILE, TILE), TILE)
            out = (pacc[mine, :] + precv[span(t), :]).astype(BF16)
            xb[c, span(t), :] = (xb[c, span(t), :].astype(F32) + out.astype(F32)).astype(BF16)

        swap_state(xb, 1).start()

        @pl.when(primary)
        def _():
            to_sib(1, 0).wait_send()
            to_sib(1, 1).wait_send()

        @pl.when(jnp.logical_not(primary))
        def _():
            for which in range(2):
                to_sib(1, which).wait_recv()
                to_pair(which).wait_send()

        turned(lambda t: seq_tile(dyb, t), dT)
        clear()
        swap_state(xb, 1).wait_send()
        remote(xb.at[1 - c], xb.at[1 - c], ex_send.at[1], ex_recv.at[1], sib).wait_recv()
        norm(xb, a1)
        turned(lambda t: a1[span(t), :], aT)
        gather(1, 5)

        def backward(l, j, a_all, with_da):
            @pl.loop(0, subs)
            def _(i):
                @pl.loop(0, tiles)
                def _(t):
                    a = a_all[span(t), :]
                    wg, wu, wd = flat(w_gate(l, j, i)), flat(w_up(l, j, i)), flat(w_down(l, j, i))
                    gate, up = nn(a, wg), nn(a, wu)
                    dact = nt(seq_tile(dyb, t), wd).astype(BF16).astype(F32)
                    sig = jax.nn.sigmoid(gate)
                    silu = gate * sig
                    actb[span(t), :] = (silu * up).astype(BF16)
                    du = (dact * silu).astype(BF16)
                    dg = (dact * up * (sig + silu * (1.0 - sig))).astype(BF16)
                    dub[span(t), :] = du
                    dgb[span(t), :] = dg
                    if with_da:
                        pacc[span(t), :] += nt(dg, wg) + nt(du, wu)

                shape = (n, n, rows, SUB)
                w_gate(l, j, i)[...] = nn(aT[...], dgb[...]).astype(BF16).reshape(shape)
                w_up(l, j, i)[...] = nn(aT[...], dub[...]).astype(BF16).reshape(shape)
                w_down(l, j, i)[...] = nn(dT[...], actb[...]).T.astype(BF16).reshape(per_sub, deep, dim)

        def where(k):
            return 1 - k // n, (x + k) % n, k % SLOTS

        half_cols, half_rows = chunk, deep // 2

        def own(b, l, j, block, half):
            if b == 0:
                return GU.at[l, :, block, :, pl.ds(pl.multiple_of(j * 2 * chunk + half * chunk, chunk), chunk)]
            return D.at[l, j, block, pl.ds(half * half_rows, half_rows), :]

        ym, yp, y2 = (y + n - 1) % n, (y + 1) % n, (y + 2) % n
        slots = (RG, RD)

        def y_copy(b, src, s, way, kind):
            dst = slots[b].at[s, way, kind]
            return remote(src, dst, y_send.at[s, way, kind, b], y_recv.at[s, way, kind, b], hop(1, -1 if way == 0 else 1))

        def raw(k):
            l, j, s = where(k)
            for way, (near, half_far, half_near) in enumerate(((ym, 0, 1), (yp, 1, 0))):
                for b in range(2):
                    yield y_copy(b, own(b, l, j, y2, half_far), s, way, 0)
                    yield y_copy(b, own(b, l, j, near, half_near), s, way, 1)

        def onward(k):
            l, j, s = where(k)
            for way in range(2):
                for b in range(2):
                    yield y_copy(b, slots[b].at[s, way, 0], s, way, 2)

        def step1(k):
            @pl.when(k >= SLOTS)
            def _():
                pl.semaphore_wait(credit.at[0], 1)
                pl.semaphore_wait(credit.at[1], 1)

            for one in raw(k):
                one.start()

        def step2(k):
            l, j, s = where(k)
            for way, (near, half) in enumerate(((ym, 0), (yp, 1))):
                for b in range(2):
                    slot = slots[b].at[s, way, 0]
                    y_copy(b, slot, s, way, 0).wait_recv()
                    slot[...] = (slot[...].astype(F32) + own(b, l, j, near, half)[...].astype(F32)).astype(BF16)
            for one in onward(k):
                one.start()

        src_id = x // 2

        def outs(k, o):
            l, j, _ = where(k)
            st = k % 2
            there = (x + o) % n
            cols = pl.ds(pl.multiple_of(j * 2 * chunk, 2 * chunk), 2 * chunk)
            return (SGU.at[st, there], pgu.at[src_id, c, l, :, cols], x_send.at[st, o], p_recv.at[src_id, c], at(there, y, role))

        def outs_d(k, o):
            l, j, _ = where(k)
            st = k % 2
            return (SD.at[st], pd.at[src_id, c, l], x_send.at[st, n], pd_recv.at[src_id, c], at((x + o) % n, y, role))

        def each_out(k, act_remote, act_local):
            for o in range(n):
                if o == 0:

                    @pl.when(primary)
                    def _():
                        act_local(pltpu.make_async_copy(*outs(k, 0)[:3]))

                        @pl.when(k % n == 0)
                        def _():
                            act_local(pltpu.make_async_copy(*outs_d(k, 0)[:3]))

                    @pl.when(jnp.logical_not(primary))
                    def _():
                        act_remote(remote(*outs(k, 0)))

                        @pl.when(k % n == 0)
                        def _():
                            act_remote(remote(*outs_d(k, 0)))

                else:
                    act_remote(remote(*outs(k, o)))

                    @pl.when(k % n == o)
                    def _():
                        act_remote(remote(*outs_d(k, o)))

        def outs_done(k):
            each_out(k, lambda d: d.wait_send(), lambda d: d.wait())

        def step3(k):
            l, j, s = where(k)
            st = k % 2
            for way in range(2):
                for b in range(2):
                    for kind in (1, 2):
                        y_copy(b, slots[b].at[s, way, 0], s, way, kind).wait_recv()

            @pl.when(k >= 2)
            def _():
                outs_done(k - 2)

            for half in range(2):
                via, direct = half, 1 - half
                summed = own(0, l, j, y, half)[...].astype(F32) + RG[s, via, 2].astype(F32) + RG[s, direct, 1].astype(F32)
                SGU[st, :, :, pl.ds(half * chunk, chunk)] = summed
                summed = own(1, l, j, y, half)[...].astype(F32) + RD[s, via, 2].astype(F32) + RD[s, direct, 1].astype(F32)
                SD[st, pl.ds(half * half_rows, half_rows), :] = summed
            each_out(k, lambda d: d.start(), lambda d: d.start())
            for one in (*raw(k), *onward(k)):
                one.wait_send()

            @pl.when(k + SLOTS < last)
            def _():
                pl.semaphore_signal(credit.at[1], inc=1, device_id=hop(1, 1), device_id_type=MESH)
                pl.semaphore_signal(credit.at[0], inc=1, device_id=hop(1, -1), device_id_type=MESH)

        @pl.loop(0, last + 2)
        def _(k):
            @pl.when(k < n)
            def _():
                backward(1, (x + k) % n, a1, True)

            @pl.when(k == n)
            def _():
                swap_partial().start()
                turned(lambda t: a0[span(t), :], aT)
                swap_partial().wait()

                @pl.loop(0, tiles_seq)
                def _(t):
                    mine = pl.ds(pl.multiple_of(c * tokens + t * TILE, TILE), TILE)
                    da = (pacc[mine, :] + precv[span(t), :]).astype(BF16).astype(F32)
                    wide = xb[c, span(t), :].astype(F32)
                    scale = scale_of(wide)
                    dh = da * scale - wide * (scale * scale * scale * jnp.mean(da * wide, -1, keepdims=True))
                    dyb[c, span(t), :] = (dyb[c, span(t), :].astype(F32) + dh.astype(BF16).astype(F32)).astype(BF16)

                swap_state(dyb, 2).start()
                swap_state(dyb, 2).wait_send()
                remote(dyb.at[1 - c], dyb.at[1 - c], ex_send.at[2], ex_recv.at[2], sib).wait_recv()
                turned(lambda t: seq_tile(dyb, t), dT)

            @pl.when(jnp.logical_and(k >= n, k < last))
            def _():
                backward(0, (x + k) % n, a0, False)

            @pl.when(k < last)
            def _():
                step1(k)

            @pl.when(jnp.logical_and(k >= 1, k <= last))
            def _():
                step2(k - 1)

            @pl.when(k >= 2)
            def _():
                step3(k - 2)

        outs_done(last - 2)
        outs_done(last - 1)
        for src in range(2):
            for core in range(2):

                @pl.when(jnp.logical_not(jnp.logical_and(primary, jnp.logical_and(src_id == src, c == core))))
                def _(src=src, core=core):
                    remote(pgu.at[src, core], pgu.at[src, core], x_send.at[0, 0], p_recv.at[src, core], sib).wait_recv()
                    remote(pd.at[src, core], pd.at[src, core], x_send.at[0, 0], pd_recv.at[src, core], sib).wait_recv()

    return kernel


def solution(mesh):
    n = math.isqrt(mesh.shape["dp"])

    def partial_sums(x, dy, w_gate, w_up, w_down):
        tokens, dim = x.shape[1:]
        layers, rows, hidden = w_gate.shape
        deep = w_down.shape[1] // 2
        cols = hidden
        chunk = hidden // 2 // n
        total = 2 * tokens
        dma = pltpu.SemaphoreType.DMA
        scratch = [
            pltpu.VMEM((layers, n, n, rows, cols), BF16),
            pltpu.VMEM((layers, n, n, deep, dim), BF16),
            pltpu.VMEM((SLOTS, 2, 3, n, rows, chunk), BF16),
            pltpu.VMEM((SLOTS, 2, 3, deep // 2, dim), BF16),
            pltpu.VMEM((2, tokens, dim), BF16),
            pltpu.VMEM((2, tokens, dim), BF16),
            pltpu.VMEM((total, dim), BF16),
            pltpu.VMEM((total, dim), BF16),
            pltpu.VMEM((dim, total), BF16),
            pltpu.VMEM((dim, total), BF16),
            pltpu.VMEM((total, dim), F32),
            pltpu.VMEM((tokens, dim), F32),
            pltpu.VMEM((total, SUB), BF16),
            pltpu.VMEM((total, SUB), BF16),
            pltpu.VMEM((total, SUB), BF16),
            pltpu.VMEM((2, n, rows, 2 * chunk), F32),
            pltpu.VMEM((2, deep, dim), F32),
            dma((layers, 2)),
            dma((2,)),
            dma((2, 2)),
            dma((2, 2)),
            dma((layers, 4, 2)),
            dma((layers, 2, 15, 2)),
            dma((3,)),
            dma((3,)),
            dma((SLOTS, 2, 3, 2)),
            dma((SLOTS, 2, 3, 2)),
            pltpu.SemaphoreType.REGULAR((2,)),
            dma((2, n + 1)),
            dma((2, 2)),
            dma((2, 2)),
        ]
        return pl.pallas_call(
            make_kernel(n, tokens, dim, rows, cols, deep, layers),
            out_shape=(
                jax.ShapeDtypeStruct((2, 2, layers, rows, cols), F32),
                jax.ShapeDtypeStruct((2, 2, layers, deep, dim), F32),
            ),
            in_specs=[pl.BlockSpec(memory_space=pl.ANY)] * 5,
            out_specs=(pl.BlockSpec(memory_space=pl.ANY),) * 2,
            scratch_shapes=scratch,
            compiler_params=pltpu.CompilerParams(collective_id=0, has_side_effects=True, vmem_limit_bytes=67043328),
        )(x, dy, w_gate, w_up, w_down)

    def step(x, dy, *arrays):
        weights, m, v = (arrays[i : i + 3] for i in (0, 3, 6))
        layers, rows, hidden = weights[0].shape
        deep, dim = weights[2].shape[1] // 2, weights[2].shape[2]
        wide, down = partial_sums(x, dy, *weights)
        wide = wide.sum(0).reshape(2, layers, rows, n, 2, n, deep)
        wide = wide.transpose(4, 1, 2, 3, 5, 0, 6).reshape(2, layers, rows, hidden)
        down = down.sum(0).transpose(1, 0, 2, 3).reshape(layers, 2 * deep, dim)
        gradients = [g.astype(BF16).astype(F32) for g in (wide[0], wide[1], down)]
        new = [adamw(w.astype(F32), m, v, g) for w, m, v, g in zip(weights, m, v, gradients, strict=True)]
        return tuple(one[which] for which in range(3) for one in new)

    states, cut = P(("rep", "dp"), None, None), P(None, "dp", None)
    return jax.shard_map(
        step,
        mesh=mesh,
        in_specs=(states, states) + (cut,) * 9,
        out_specs=(P("rep", "dp", None),) * 9,
        check_vma=False,
    )
```

time: 1020 us -> 477 us (0.47)
  waiting for transfers between devices: 641 us -> 0 us
  Pallas kernels: 0 us -> 432 us
  matrix products: 331 us -> 0 us
  between operations: 15 us -> 0.75 us
  local copies, waits for them, and re-layouts: 11 us -> 22.7 us
    pallas_call x0 -> x1, Pallas kernels: none -> 432 us  [partial_sums(): pl.pallas_call(make_kernel(n, tokens, dim, rows, cols, deep, layers), out...]
    reduce_scatter x6 -> x0, waiting for transfers between devices: 340 us -> none  [step(): lax.psum_scatter(by_w[name], 'dp', scatter_dimension=0, tiled=True)]
    dot_general x15 -> x0, matrix products: 331 us -> none  [the longest x5 123 us: layer(): gate = jnp.dot(a, w['w_gate'], preferred_element_type=jnp.float32)]
    all_gather x6 -> x0, waiting for transfers between devices: 298 us -> none  [fetched(): lax.all_gather(w[number], 'dp', axis=0, tiled=True)]
    convert_element_type x0 -> x5, local copies, waits for them, and re-layouts: none -> 15.9 us  [step(): gradients = [g.astype(BF16).astype(F32) for g in (wide[0], wide[1], down)]]
  transfers between devices with their start and end apart: 12 -> 0, of which waited for: 11 -> 0; matrix products, arithmetic and copies ran while one was open for 25% -> 0% of each run, Pallas kernels for 0% -> 0%
where the time goes in v1:
time: 477 us
  Pallas kernels  432 us (91%)
  local copies, waits for them, and re-layouts  22.7 us (5%)
  other arithmetic  21.5 us (5%)
    pallas_call x1, Pallas kernels, partial_sums(): pl.pallas_call(make_kernel(n, tokens, dim, rows, cols, deep, layers), out...  432 us
    convert_element_type x5, local copies, waits for them, and re-layouts, step(): gradients = [g.astype(BF16).astype(F32) for g in (wide[0], wide[1], down)]  15.9 us
    convert_element_type x2, other arithmetic, adamw(): return ((w - 0.02 * step).astype(BF16), m, v)  10.7 us

profile of v1, /device:TPU:97, one launch (start us, length us, event | category | flops | bytes accessed | tf_op | source)
XLA Modules:
  0.0 477.2 jit_solution(13366715421176734286)
XLA Ops:
  0.6 432.2 %shard_map.178 = (f32[2,2,2,32,8192]{4,3,2,1,0:T(8,128)}, f32[2,2,2,256,512]{4,3,2,1,0:T(8,128)}) custom-call(bf16[1,1024,512]{2,1,0:T(8,128)(2,1)} %x_ref.1, bf16[1,1024,512]{2,1,0:T(8,128)(2,1)} %dy_ref.1, bf16[2,32,8192]{2,1,0:T(8,128)(2,1)} %wg_ref.1, bf16[2,32,8192]{2,1,0:T(8,128)(2,1)} %wu_ref.1, bf16[2,512,512]{2,1,0:T(8,128)(2,1)} %wd_ref.1), custom_call_target="tpu_custom_call" | custom-call | tf_op jit(solution)/shard_map/pallas_call | solution.py:579
  432.9 5.9 %reduce_sum.18 = bf16[2,2,32,8192]{3,2,1,0:T(8,128)(2,1)} reduce(f32[2,2,2,32,8192]{4,3,2,1,0:T(8,128)} %get-tuple-element.11, f32[]{:T(128)} %constant.8.clone.1), dimensions={0}, to_apply=%region_0.0 | reduce | flops 1048576 | bytes 10485764 | tf_op jit(solution)/shard_map/reduce_sum | solution.py:596
  438.8 2.8 reduce_sum.19
  441.6 3.5 reshape.40
  445.2 1.2 copy.32
  446.4 0.3 convert_bitcast_fusion
  446.6 1.5 copy.30
  448.1 1.8 slice_convert_fusion
  449.9 2.9 copy.29
  452.9 2.9 reshape.38
  455.8 4.5 copy.28
  460.4 0.0 copy-start.1
  460.4 4.0 reshape.37
  464.3 0.0 copy-done.1
  464.3 0.0 copy-start
  464.3 0.0 copy-start.2
  464.3 0.0 copy-start.3
  464.3 0.0 copy-start.4
  464.4 0.0 copy-start.5
  464.4 0.0 copy-start.6
  464.4 0.0 copy-start.7
  464.4 6.2 %fusion.8 = (bf16[2,512,512]{2,1,0:T(8,128)(2,1)}, f32[2,512,512]{2,1,0:T(8,128)}, f32[2,512,512]{2,1,0:T(8,128)}) fusion(bf16[2,512,512]{2,1,0:T(8,128)(2,1)S(1)} %copy-done.1, f32[2,2,256,512]{3,2,1,0:T(8,128)} %copy.30, f32[2,512,512]{2,1,0:T(8,128)} %param.21, f32[2,512,512]{2,1,0:T(8,128)} %param.18), kind=kLoop, calls=%fused_computation.17 | loop fusion | flops 7864320 | bytes 12582912 | tf_op jit(solution)/shard_map/convert_element_type | solution.py:21
  470.6 0.0 copy-done
  470.6 0.0 copy-done.2
  470.6 0.0 copy-done.3
  470.6 0.0 copy-done.4
  470.6 0.6 copy-done.5
  471.3 0.8 copy-done.6
  472.1 0.6 copy-done.7
  472.7 4.5 fusion.2
Async XLA Ops:
  460.4 4.0 copy-start.1
  464.3 6.3 %copy-start = (f32[2,32,8192]{2,1,0:T(8,128)S(1)}, f32[2,32,8192]{2,1,0:T(8,128)}, u32[]{:S(2)}) copy-start(f32[2,32,8192]{2,1,0:T(8,128)} %reshape.37) | copy-start | bytes 6291460
  464.3 6.3 %copy-start.2 = (bf16[2,32,8192]{2,1,0:T(8,128)(2,1)S(1)}, bf16[2,32,8192]{2,1,0:T(8,128)(2,1)}, u32[]{:S(2)}) copy-start(bf16[2,32,8192]{2,1,0:T(8,128)(2,1)} %wg_ref.1) | copy-start | bytes 3145732
  464.3 6.3 %copy-start.3 = (bf16[2,32,8192]{2,1,0:T(8,128)(2,1)S(1)}, bf16[2,32,8192]{2,1,0:T(8,128)(2,1)}, u32[]{:S(2)}) copy-start(bf16[2,32,8192]{2,1,0:T(8,128)(2,1)} %wu_ref.1) | copy-start | bytes 3145732
  464.3 6.3 %copy-start.4 = (f32[2,32,8192]{2,1,0:T(8,128)S(1)}, f32[2,32,8192]{2,1,0:T(8,128)}, u32[]{:S(2)}) copy-start(f32[2,32,8192]{2,1,0:T(8,128)} %param.19) | copy-start | bytes 6291460
  464.4 6.9 %copy-start.5 = (f32[2,32,8192]{2,1,0:T(8,128)S(1)}, f32[2,32,8192]{2,1,0:T(8,128)}, u32[]{:S(2)}) copy-start(f32[2,32,8192]{2,1,0:T(8,128)} %param.16) | copy-start | bytes 6291460
  464.4 7.8 %copy-start.6 = (f32[2,32,8192]{2,1,0:T(8,128)S(1)}, f32[2,32,8192]{2,1,0:T(8,128)}, u32[]{:S(2)}) copy-start(f32[2,32,8192]{2,1,0:T(8,128)} %param.20) | copy-start | bytes 6291460
  464.4 8.3 %copy-start.7 = (f32[2,32,8192]{2,1,0:T(8,128)S(1)}, f32[2,32,8192]{2,1,0:T(8,128)}, u32[]{:S(2)}) copy-start(f32[2,32,8192]{2,1,0:T(8,128)} %param.17) | copy-start | bytes 6291460

commit v2 on v1

v2 whole, which is shorter than its diff:
```python
import math

import jax
import jax.numpy as jnp
from jax import lax
from jax.experimental import pallas as pl
from jax.experimental.pallas import tpu as pltpu
from jax.sharding import PartitionSpec as P

MESH = pl.DeviceIdType.MESH
BF16, F32 = jnp.bfloat16, jnp.float32
TILE = 512
SLOTS = 3


def adamw(w, m, v, g):
    m = 0.9 * m + 0.1 * g
    v = 0.95 * v + 0.05 * g * g
    step = m * lax.rsqrt(v + 1e-8) + 0.1 * w
    return (w - 0.02 * step).astype(BF16), m, v


def nn(a, b):
    return lax.dot_general(a, b, (((1,), (0,)), ((), ())), preferred_element_type=F32)


def nt(a, b):
    return lax.dot_general(a, b, (((1,), (1,)), ((), ())), preferred_element_type=F32)


def sigmoid(a):
    return 0.5 * jnp.tanh(0.5 * a) + 0.5


def scale_of(wide):
    return lax.rsqrt(jnp.mean(wide * wide, -1, keepdims=True) + 1e-6)


def make_kernel(n, tokens, dim, rows, wide_cols, deep, layers):
    total = 2 * tokens
    part = deep // 2
    sub = n * part
    wide = wide_cols // 2
    subs = n // 2
    span_cols = 2 * sub * subs
    chunk = span_cols // 2
    tiles = total // TILE
    tiles_seq = tokens // TILE
    last = layers * n

    def kernel(
        x_ref, dy_ref, wg_ref, wu_ref, wd_ref, far_g, near_g, far_d, near_d,
        GU, D, RG, RD, RX, xb, dyb, a0, a1, aT, dT, pacc, precv, actb, dgb, dub, SB, S32, SDB, SD32,
        ld_sem, q_loc, q_send, q_recv, ag_send, ag_recv, ex_send, ex_recv, y_send, y_recv, m_send, m_recv, credit, x_send, xd_send, p_recv, pd_recv,
    ):
        rep, dp = lax.axis_index("rep"), lax.axis_index("dp")
        c, base = rep % 2, (rep // 2) * 2
        x, y = dp // n, dp % n
        role = x // (n // 2)
        pair, mate = n - 1 - x, x + 1 - 2 * (x % 2)
        sib = (base + 1 - c, dp)

        def at(px, py, core=None):
            return (base + (c if core is None else core), px * n + py)

        def hop(axis, sign):
            return at((x + sign) % n, y) if axis == 0 else at(x, (y + sign) % n)

        for l in range(layers):

            @pl.loop(0, n * n)
            def _(d, l=l):
                for m, w in enumerate((wg_ref, wu_ref)):
                    for h in range(2):
                        to = h * wide + (d // n) * 2 * sub + m * sub + (d % n) * part
                        pltpu.make_async_copy(
                            w.at[l, :, pl.ds(pl.multiple_of(d * 2 * deep + c * deep + h * part, part), part)],
                            GU.at[l, x, y, :, pl.ds(pl.multiple_of(to, part), part)],
                            ld_sem.at[l, 0],
                        ).start()

            for h in range(2):
                rows_h = pl.ds(pl.multiple_of(c * deep + h * part, part), part)
                pltpu.make_async_copy(wd_ref.at[l, rows_h, :], D.at[l, h, x, y], ld_sem.at[l, 1]).start()

        def own_loaded(l):
            pltpu.make_async_copy(GU.at[l, x, y], GU.at[l, x, y], ld_sem.at[l, 0]).wait()
            pltpu.make_async_copy(D.at[l, :, x, y], D.at[l, :, x, y], ld_sem.at[l, 1]).wait()

        barrier = pltpu.get_barrier_semaphore()
        friends = [sib, hop(1, 1), hop(1, -1)]
        for o in range(1, n):
            for core in range(2):
                friends.append(at((x + o) % n, y, core))
        for f in friends:
            pl.semaphore_signal(barrier, inc=1, device_id=f, device_id_type=MESH)
        pl.semaphore_wait(barrier, len(friends))

        def remote(src, dst, ss, rs, dev):
            return pltpu.make_async_remote_copy(src_ref=src, dst_ref=dst, send_sem=ss, recv_sem=rs, device_id=dev, device_id_type=MESH)

        def piece(b, g, path, p, q, half):
            l, h = g // 2, g % 2
            px, py = (p, q) if path == 0 else (q, p)
            if b == 0:
                at_cols = pl.ds(h * wide, wide) if half is None else pl.ds(h * wide + half * (wide // 2), wide // 2)
                return GU.at[l, px, py, pl.ds(path * (rows // 2), rows // 2), at_cols]
            first, count = path * (part // 2), part // 2
            if half is not None:
                first, count = first + half * (count // 2), count // 2
            return D.at[l, h, px, py, pl.ds(first, count), :]

        def blocks(b, g, which):
            if b == 0:
                return GU.at[(g // 2, *which, slice(None), pl.ds((g % 2) * wide, wide))]
            return D.at[(g // 2, g % 2, *which)]

        def moved(l, path, p, q, half, axis, sign, cls, ev):
            dev = hop(axis if path == 0 else 1 - axis, sign)
            return [
                remote(piece(b, l, path, p, q, half), piece(b, l, path, p, q, half), ag_send.at[l, cls, b], ag_recv.at[l, path, ev, b], dev)
                for b in range(2)
            ]

        def send(*args):
            for one in moved(*args):
                one.start()

        def arrived(l, path, p, q, half, ev):
            for one in moved(l, path, p, q, half, 0, 1, 0, ev):
                one.wait_recv()

        paths = ((0, x, y), (1, y, x))

        def spread(g, path, p, q, half, cls, ev):
            send(g, path, p, q, half, 1, 1, cls, ev)
            send(g, path, p, q, half, 1, -1, cls, ev + 5)

        def relay(g, path, p, ends, whole, ev, step):
            for half, sign in enumerate((1, -1)):
                arrived(g, path, p, ends[half], None if whole else half, ev + step * half)
                send(g, path, p, ends[half], half, 1, sign, 3, 14)

        def gather(g, stage):
            for path, p, q in paths:
                sides, across, ends = ((p + n - 1) % n, (p + 1) % n), (p + 2) % n, ((q + n - 1) % n, (q + 1) % n)
                if stage == 0:
                    for half, sign in enumerate((1, -1)):
                        send(g, path, p, q, None, 0, sign, 0, half)
                    spread(g, path, p, q, None, 0, 4)
                if stage == 1:
                    for half, sign in enumerate((1, -1)):
                        arrived(g, path, sides[half], q, None, half)
                        send(g, path, sides[half], q, half, 0, sign, 2, 2 + half)
                        spread(g, path, sides[half], q, None, 0, 5 + half)
                if stage == 2:
                    relay(g, path, p, ends, True, 4, 5)
                    for half in range(2):
                        arrived(g, path, across, q, half, 2 + half)
                        spread(g, path, across, q, half, 1, 7 + half)
                if stage == 3:
                    for half in range(2):
                        relay(g, path, sides[half], ends, True, 5 + half, 5)
                if stage == 4:
                    relay(g, path, across, ends, False, 7, 6)
                    for half in range(2):
                        arrived(g, path, across, ends[half], 1 - half, 8 + 4 * half)
                if stage == 5:
                    for b in range(2):
                        size = blocks(b, g, (0, pl.ds(0, 2)))
                        remote(size, size, ag_send.at[g, 0, b], ag_recv.at[g, path, 14, b], sib).wait_recv()
            if stage == 5:
                every = slice(None)
                for b in range(2):
                    for cls, which in enumerate(((pl.ds(0, 2), every), (0, pl.ds(0, 2)), (0, 0), (0, every))):
                        size = blocks(b, g, which)
                        remote(size, size, ag_send.at[g, cls, b], ag_recv.at[g, 0, 0, b], sib).wait_send()

        primary = c == role
        inputs = ((x_ref, xb), (dy_ref, dyb))

        def to_pair(w):
            src, buf = inputs[w]
            return remote(src.at[0], buf.at[role], q_send.at[w, 0], q_recv.at[w, 1], at(pair, y))

        def to_sib(w, which):
            buf = inputs[w][1]
            slot = role if which == 0 else 1 - role
            return remote(buf.at[slot], buf.at[slot], q_send.at[w, which], q_recv.at[w, which], sib)

        def local(w):
            src, buf = inputs[w]
            return pltpu.make_async_copy(src.at[0], buf.at[role], q_loc.at[w])

        @pl.when(primary)
        def _():
            local(0).start()
            local(1).start()

        own_loaded(0)
        gather(0, 0)

        @pl.when(jnp.logical_not(primary))
        def _():
            to_pair(0).start()

        @pl.when(primary)
        def _():
            for w in range(2):
                local(w).wait()
                to_sib(w, 0).start()

        gather(0, 1)
        gather(0, 2)

        @pl.when(primary)
        def _():
            to_sib(0, 1).wait_recv()
            to_sib(0, 1).start()

        gather(0, 3)
        gather(1, 0)
        gather(0, 4)

        @pl.when(jnp.logical_not(primary))
        def _():
            to_pair(1).start()
            for which in range(2):
                to_sib(0, which).wait_recv()

        @pl.when(primary)
        def _():
            to_sib(0, 0).wait_send()
            to_sib(0, 1).wait_send()

        def norm(h, a):
            @pl.loop(0, tiles)
            def _(t):
                s, r = t // tiles_seq, pl.ds(pl.multiple_of((t % tiles_seq) * TILE, TILE), TILE)
                wide = h[s, r, :].astype(F32)
                a[pl.ds(pl.multiple_of(t * TILE, TILE), TILE), :] = (wide * scale_of(wide)).astype(BF16)

        def turned(src, dst):
            @pl.loop(0, tiles)
            def _(t):
                dst[:, pl.ds(pl.multiple_of(t * TILE, TILE), TILE)] = src(t).astype(F32).T.astype(BF16)

        def span(t):
            return pl.ds(pl.multiple_of(t * TILE, TILE), TILE)

        def seq_tile(b, t):
            return b[t // tiles_seq, pl.ds(pl.multiple_of((t % tiles_seq) * TILE, TILE), TILE), :]

        norm(xb, a0)

        def clear():
            @pl.loop(0, tiles)
            def _(t):
                pacc[span(t), :] = jnp.zeros((TILE, dim), F32)

        clear()
        gather(0, 5)

        def w_gate(l, h, j):
            return GU.at[l, :, :, :, pl.ds(pl.multiple_of(h * wide + j * 2 * sub, sub), sub)]

        def w_up(l, h, j):
            return GU.at[l, :, :, :, pl.ds(pl.multiple_of(h * wide + j * 2 * sub + sub, sub), sub)]

        def w_down(l, h, j):
            return D.at[l, h, j]

        def flat(ref):
            v = ref[...]
            return v.reshape(math.prod(v.shape[:-1]), v.shape[-1])

        def swap_partial():
            part = pacc.at[pl.ds(pl.multiple_of((1 - c) * tokens, tokens), tokens), :]
            return remote(part, precv, ex_send.at[0], ex_recv.at[0], sib)

        def swap_state(buf, which):
            return remote(buf.at[c], buf.at[c], ex_send.at[which], ex_recv.at[which], sib)

        for h in range(2):

            @pl.loop(0, tiles)
            def _(t0, h=h):
                t = (t0 + (1 - c) * tiles_seq) % tiles

                @pl.loop(0, n)
                def _(j):
                    a = a0[span(t), :]
                    gate = nn(a, flat(w_gate(0, h, j)))
                    up = nn(a, flat(w_up(0, h, j)))
                    act = (gate * sigmoid(gate) * up).astype(BF16)
                    pacc[span(t), :] += nn(act, flat(w_down(0, h, j)))

                if h == 1:

                    @pl.when(t0 == tiles_seq - 1)
                    def _():
                        swap_partial().start()

                for stage in range(1, 5):

                    @pl.when(t0 == (stage - 1) * tiles // 4)
                    def _(stage=stage):
                        gather(1 + h, stage)
                        if stage == 3:
                            if h == 0:
                                own_loaded(1)
                            gather(2 + h, 0)

            if h == 0:
                gather(1, 5)

        @pl.when(primary)
        def _():
            to_sib(1, 1).wait_recv()
            to_sib(1, 1).start()

        swap_partial().wait()

        @pl.loop(0, tiles_seq)
        def _(t):
            mine = pl.ds(pl.multiple_of(c * tokens + t * TILE, TILE), TILE)
            out = (pacc[mine, :] + precv[span(t), :]).astype(BF16)
            xb[c, span(t), :] = (xb[c, span(t), :].astype(F32) + out.astype(F32)).astype(BF16)

        swap_state(xb, 1).start()

        @pl.when(primary)
        def _():
            to_sib(1, 0).wait_send()
            to_sib(1, 1).wait_send()

        @pl.when(jnp.logical_not(primary))
        def _():
            for which in range(2):
                to_sib(1, which).wait_recv()
                to_pair(which).wait_send()

        turned(lambda t: seq_tile(dyb, t), dT)
        clear()
        swap_state(xb, 1).wait_send()
        remote(xb.at[1 - c], xb.at[1 - c], ex_send.at[1], ex_recv.at[1], sib).wait_recv()
        norm(xb, a1)
        turned(lambda t: a1[span(t), :], aT)
        gather(2, 5)

        def where(k):
            return 1 - k // n, (k % n) // 2, k % 2, k % SLOTS

        def own(b, k, block, half, px=None):
            l, h, jj, _ = where(k)
            if b == 0:
                cols = pl.ds(pl.multiple_of(h * wide + jj * span_cols + half * chunk, chunk), chunk)
                return GU.at[l, slice(None) if px is None else px, block, :, cols]
            return D.at[l, h, kept_x(k), block, pl.ds(half * (part // 2), part // 2), :]

        def kept_x(k):
            jj = k % 2
            same = 1 - (x // subs + jj) % 2
            return same * x + (1 - same) * pair

        def given_x(k):
            return 2 * subs * (k % 2) + 1 - kept_x(k)

        def to_mate(k):
            l, h, _, s = where(k)
            return remote(D.at[l, h, given_x(k)], RX.at[s], m_send.at[s], m_recv.at[s], at(mate, y))

        def from_mate(k, block, half):
            return RX.at[k % SLOTS, block, pl.ds(half * (part // 2), part // 2), :]

        def backward(l, k, a_all, with_da):
            h = (k % n) // 2

            @pl.loop(0, subs)
            def _(i):
                j = i * kept_x(k) + (1 - i) * given_x(k)

                @pl.loop(0, tiles)
                def _(t):
                    a = a_all[span(t), :]
                    wg, wu, wd = flat(w_gate(l, h, j)), flat(w_up(l, h, j)), flat(w_down(l, h, j))
                    gate, up = nn(a, wg), nn(a, wu)
                    dact = nt(seq_tile(dyb, t), wd).astype(BF16).astype(F32)
                    sig = sigmoid(gate)
                    silu = gate * sig
                    actb[span(t), :] = (silu * up).astype(BF16)
                    du = (dact * silu).astype(BF16)
                    dg = (dact * up * (sig + silu * (1.0 - sig))).astype(BF16)
                    dub[span(t), :] = du
                    dgb[span(t), :] = dg
                    if with_da:
                        pacc[span(t), :] += nt(dg, wg) + nt(du, wu)

                shape = (n, n, rows, sub)
                w_gate(l, h, j)[...] = nn(aT[...], dgb[...]).astype(BF16).reshape(shape)
                w_up(l, h, j)[...] = nn(aT[...], dub[...]).astype(BF16).reshape(shape)
                w_down(l, h, j)[...] = nn(dT[...], actb[...]).T.astype(BF16).reshape(n, part, dim)

                @pl.when(i == 0)
                def _():
                    @pl.when(k >= SLOTS)
                    def _():
                        pl.semaphore_wait(credit.at[2], 1)

                    to_mate(k).start()

                    @pl.when(k >= 1)
                    def _():
                        step2(k - 1)

                if l == 1:
                    for stage in range(1, 5):

                        @pl.when(k * subs + i == stage - 1)
                        def _(stage=stage):
                            gather(3, stage)

        ym, yp, y2 = (y + n - 1) % n, (y + 1) % n, (y + 2) % n
        slots = (RG, RD)

        def y_copy(b, src, s, way, kind):
            dst = slots[b].at[s, way, kind]
            return remote(src, dst, y_send.at[s, way, kind, b], y_recv.at[s, way, kind, b], hop(1, -1 if way == 0 else 1))

        def raw(b, k):
            s = k % SLOTS
            source = own if b == 0 else lambda _, k, block, half: from_mate(k, block, half)
            for way, (near, half_far, half_near) in enumerate(((ym, 0, 1), (yp, 1, 0))):
                yield y_copy(b, source(b, k, y2, half_far), s, way, 0)
                yield y_copy(b, source(b, k, near, half_near), s, way, 1)

        def onward(k):
            s = k % SLOTS
            for way in range(2):
                for b in range(2):
                    yield y_copy(b, slots[b].at[s, way, 0], s, way, 2)

        def step1(k):
            @pl.when(k >= SLOTS)
            def _():
                pl.semaphore_wait(credit.at[0], 1)
                pl.semaphore_wait(credit.at[1], 1)

            for one in raw(0, k):
                one.start()

        def term(b, k, block, half, px=None):
            mine = own(b, k, block, half, px)[...].astype(F32)
            return mine if b == 0 else mine + from_mate(k, block, half)[...].astype(F32)

        def step1_down(k):
            to_mate(k).wait_recv()
            for block, half in ((y2, 0), (y2, 1), (ym, 1), (yp, 0)):
                from_mate(k, block, half)[...] = term(1, k, block, half).astype(BF16)
            for one in raw(1, k):
                one.start()

        def step2(k):
            s = k % SLOTS
            for way, (near, half) in enumerate(((ym, 0), (yp, 1))):
                for b in range(2):
                    slot = slots[b].at[s, way, 0]
                    y_copy(b, slot, s, way, 0).wait_recv()
                    slot[...] = (slot[...].astype(F32) + term(b, k, near, half)).astype(BF16)
            for one in onward(k):
                one.start()

        def near_out(k, src, dst, ss, rs, act_remote, act_local):
            @pl.when(primary)
            def _():
                act_local(pltpu.make_async_copy(src, dst, ss))

            @pl.when(jnp.logical_not(primary))
            def _():
                act_remote(remote(src, dst, ss, rs, sib))

        def each_out(k, act_remote, act_local):
            l, h, jj, _ = where(k)
            st = k % 2
            cols = pl.ds(pl.multiple_of(h * wide + jj * span_cols, span_cols), span_cols)
            near_out(k, S32.at[st], near_g.at[c, l, :, cols], x_send.at[st, 0], p_recv.at[2, c], act_remote, act_local)
            for o in range(1, n):
                there, far = (x + o) % n, int(o == 2)
                act_remote(remote(SB.at[st, there], far_g.at[far, c, l, :, cols], x_send.at[st, o], p_recv.at[far, c], at(there, y, role)))
            at_rows = pl.ds(pl.multiple_of(c * deep + h * part, part), part)
            here = x // subs == jj

            @pl.when(here)
            def _():
                near_out(k, SD32.at[st], near_d.at[l, at_rows], xd_send.at[st], pd_recv.at[1, c], act_remote, act_local)

            @pl.when(jnp.logical_not(here))
            def _():
                act_remote(remote(SDB.at[st], far_d.at[l, at_rows], xd_send.at[st], pd_recv.at[0, c], at(pair, y, role)))

        def outs_done(k):
            each_out(k, lambda d: d.wait_send(), lambda d: d.wait())

        def step3(k):
            s, st = k % SLOTS, k % 2
            for way in range(2):
                for b in range(2):
                    for kind in (1, 2):
                        y_copy(b, slots[b].at[s, way, 0], s, way, kind).wait_recv()

            @pl.when(k >= 2)
            def _():
                outs_done(k - 2)

            for half in range(2):
                via, direct = half, 1 - half
                cols = pl.ds(half * chunk, chunk)
                for px in range(n):
                    summed = own(0, k, y, half, px)[...].astype(F32) + RG[s, via, 2, px].astype(F32) + RG[s, direct, 1, px].astype(F32)
                    SB[st, px, :, cols] = summed.astype(BF16)

                    @pl.when(x == px)
                    def _(summed=summed, cols=cols):
                        S32[st, :, cols] = summed

                summed = term(1, k, y, half) + RD[s, via, 2].astype(F32) + RD[s, direct, 1].astype(F32)
                at_rows = pl.ds(half * (part // 2), part // 2)
                SDB[st, at_rows, :] = summed.astype(BF16)
                SD32[st, at_rows, :] = summed

            each_out(k, lambda d: d.start(), lambda d: d.start())
            for one in (*raw(0, k), *raw(1, k), *onward(k), to_mate(k)):
                one.wait_send()

            @pl.when(k + SLOTS < last)
            def _():
                pl.semaphore_signal(credit.at[1], inc=1, device_id=hop(1, 1), device_id_type=MESH)
                pl.semaphore_signal(credit.at[0], inc=1, device_id=hop(1, -1), device_id_type=MESH)
                pl.semaphore_signal(credit.at[2], inc=1, device_id=at(mate, y), device_id_type=MESH)

        @pl.loop(0, last + 1)
        def _(k):
            @pl.when(k < n)
            def _():
                @pl.when(k == 2)
                def _():
                    gather(3, 5)

                backward(1, k, a1, True)

                @pl.when(k == n - 1)
                def _():
                    swap_partial().start()

            @pl.when(k == n)
            def _():
                turned(lambda t: a0[span(t), :], aT)
                swap_partial().wait()

                @pl.loop(0, tiles_seq)
                def _(t):
                    mine = pl.ds(pl.multiple_of(c * tokens + t * TILE, TILE), TILE)
                    da = (pacc[mine, :] + precv[span(t), :]).astype(BF16).astype(F32)
                    wide = xb[c, span(t), :].astype(F32)
                    scale = scale_of(wide)
                    dh = da * scale - wide * (scale * scale * scale * jnp.mean(da * wide, -1, keepdims=True))
                    dyb[c, span(t), :] = (dyb[c, span(t), :].astype(F32) + dh.astype(BF16).astype(F32)).astype(BF16)

                swap_state(dyb, 2).start()
                swap_state(dyb, 2).wait_send()
                remote(dyb.at[1 - c], dyb.at[1 - c], ex_send.at[2], ex_recv.at[2], sib).wait_recv()
                turned(lambda t: seq_tile(dyb, t), dT)

            @pl.when(jnp.logical_and(k >= n, k < last))
            def _():
                backward(0, k, a0, False)

            @pl.when(k < last)
            def _():
                step1(k)

            @pl.when(k == last)
            def _():
                step2(k - 1)

            @pl.when(k >= 1)
            def _():
                step3(k - 1)

            @pl.when(k < last)
            def _():
                step1_down(k)

        outs_done(last - 2)
        outs_done(last - 1)

        def landed(part_of, sem):
            remote(part_of, part_of, x_send.at[0, 0], sem, sib).wait_recv()

        for core in range(2):
            landed(far_g.at[0, core], p_recv.at[0, core])

            @pl.when(jnp.logical_not(primary))
            def _(core=core):
                landed(far_g.at[1, core], p_recv.at[1, core])
                landed(far_d.at[0], pd_recv.at[0, core])

            @pl.when(jnp.logical_and(primary, c != core))
            def _(core=core):
                landed(near_g.at[core], p_recv.at[2, core])
                landed(near_d.at[0], pd_recv.at[1, core])

    return kernel


def gated_adamw(n, deep):
    part = deep // 2
    sub = n * part

    def kernel(near_ref, far_ref, g_ref, wg, mg, vg, wu, mu, vu, owg, owu, omg, omu, ovg, ovu):
        near = near_ref[0] != 0
        wide = far_ref.shape[-1] // 2
        for i, (w, m, v, ow, om, ov) in enumerate(((wg, mg, vg, owg, omg, ovg), (wu, mu, vu, owu, omu, ovu))):
            for d in range(n * n):
                for core in range(2):
                    for h in range(2):
                        first = h * wide + (d // n) * 2 * sub + i * sub + (d % n) * part
                        cols = slice(first, first + part)
                        other = jnp.where(near, g_ref[core, 0, :, cols], far_ref[1, core, 0, :, cols].astype(F32))
                        g = (far_ref[0, core, 0, :, cols].astype(F32) + other).astype(BF16).astype(F32)
                        first = d * 2 * deep + core * deep + h * part
                        cols = slice(first, first + part)
                        at = (0, slice(None), cols)
                        ow[at], om[at], ov[at] = adamw(w[at].astype(F32), m[at], v[at], g)

    return kernel


def solution(mesh):
    n = math.isqrt(mesh.shape["dp"])

    def partial_sums(x, dy, w_gate, w_up, w_down):
        tokens, dim = x.shape[1:]
        layers, rows, hidden = w_gate.shape
        deep = w_down.shape[1] // 2
        cols = hidden
        chunk = hidden // 2 // n
        part = deep // 2
        sub = n * part
        total = 2 * tokens
        dma = pltpu.SemaphoreType.DMA
        scratch = [
            pltpu.VMEM((layers, n, n, rows, cols), BF16),
            pltpu.VMEM((layers, 2, n, n, part, dim), BF16),
            pltpu.VMEM((SLOTS, 2, 3, n, rows, chunk), BF16),
            pltpu.VMEM((SLOTS, 2, 3, part // 2, dim), BF16),
            pltpu.VMEM((SLOTS, n, part, dim), BF16),
            pltpu.VMEM((2, tokens, dim), BF16),
            pltpu.VMEM((2, tokens, dim), BF16),
            pltpu.VMEM((total, dim), BF16),
            pltpu.VMEM((total, dim), BF16),
            pltpu.VMEM((dim, total), BF16),
            pltpu.VMEM((dim, total), BF16),
            pltpu.VMEM((total, dim), F32),
            pltpu.VMEM((tokens, dim), F32),
            pltpu.VMEM((total, sub), BF16),
            pltpu.VMEM((total, sub), BF16),
            pltpu.VMEM((total, sub), BF16),
            pltpu.VMEM((2, n, rows, 2 * chunk), BF16),
            pltpu.VMEM((2, rows, 2 * chunk), F32),
            pltpu.VMEM((2, part, dim), BF16),
            pltpu.VMEM((2, part, dim), F32),
            dma((layers, 2)),
            dma((2,)),
            dma((2, 2)),
            dma((2, 2)),
            dma((2 * layers, 4, 2)),
            dma((2 * layers, 2, 15, 2)),
            dma((3,)),
            dma((3,)),
            dma((SLOTS, 2, 3, 2)),
            dma((SLOTS, 2, 3, 2)),
            dma((SLOTS,)),
            dma((SLOTS,)),
            pltpu.SemaphoreType.REGULAR((3,)),
            dma((2, n)),
            dma((2,)),
            dma((3, 2)),
            dma((2, 2)),
        ]
        return pl.pallas_call(
            make_kernel(n, tokens, dim, rows, cols, deep, layers),
            out_shape=(
                jax.ShapeDtypeStruct((2, 2, layers, rows, cols), BF16),
                jax.ShapeDtypeStruct((2, layers, rows, cols), F32),
                jax.ShapeDtypeStruct((layers, 2 * deep, dim), BF16),
                jax.ShapeDtypeStruct((layers, 2 * deep, dim), F32),
            ),
            in_specs=[pl.BlockSpec(memory_space=pl.ANY)] * 5,
            out_specs=(pl.BlockSpec(memory_space=pl.ANY),) * 4,
            scratch_shapes=scratch,
            compiler_params=pltpu.CompilerParams(collective_id=0, has_side_effects=True, vmem_limit_bytes=67043328),
        )(x, dy, w_gate, w_up, w_down)

    def step(x, dy, *arrays):
        wg, wu, wd, mg, mu, md, vg, vu, vd = arrays
        layers, rows, hidden = wg.shape
        deep = wd.shape[1] // 2
        far_g, near_g, far_d, near_d = partial_sums(x, dy, wg, wu, wd)
        near = lax.axis_index("rep") % 2 == (lax.axis_index("dp") // n) // (n // 2)
        tall = 16

        def cut_rows(*lead):
            return pl.BlockSpec((*lead, 1, tall, hidden), lambda l, r: (*(0 for _ in lead), l, r, 0))

        like = [jax.ShapeDtypeStruct(one.shape, kind) for kind, one in ((BF16, wg), (F32, mg), (F32, vg)) for _ in range(2)]
        wide = pl.pallas_call(
            gated_adamw(n, deep),
            grid=(layers, rows // tall),
            out_shape=like,
            in_specs=[pl.BlockSpec(memory_space=pltpu.SMEM), cut_rows(2, 2), cut_rows(2)] + [cut_rows()] * 6,
            out_specs=[cut_rows()] * 6,
        )(near.astype(jnp.int32)[None], far_g, near_g, wg, mg, vg, wu, mu, vu)
        g = jnp.where(near, near_d, far_d.astype(F32))
        down = adamw(wd.astype(F32), md, vd, g.astype(BF16).astype(F32))
        pairs = zip(wide[::2], wide[1::2], down, strict=True)
        return tuple(one for three in pairs for one in three)

    states, cut = P(("rep", "dp"), None, None), P(None, "dp", None)
    return jax.shard_map(
        step,
        mesh=mesh,
        in_specs=(states, states) + (cut,) * 9,
        out_specs=(P("rep", "dp", None),) * 9,
        check_vma=False,
    )
```

time: 477 us -> 394 us (0.83)
  Pallas kernels: 432 us -> 388 us
  local copies, waits for them, and re-layouts: 22.7 us -> 0.01 us
  other arithmetic: 21.5 us -> 4.98 us
    pallas_call x1, Pallas kernels: 432 us -> 377 us  [partial_sums(): pl.pallas_call(make_kernel(n, tokens, dim, rows, cols, deep, layers), out...]
    convert_element_type x5 -> x0, local copies, waits for them, and re-layouts: 15.9 us -> none  [step(): gradients = [g.astype(BF16).astype(F32) for g in (wide[0], wide[1], down)]]
    pallas_call x0 -> x1, Pallas kernels: none -> 11 us  [step(): pl.pallas_call(gated_adamw(n, deep), grid=(layers, rows // tall), out_sha...]
    reduce_sum x2 -> x0, other arithmetic: 8.74 us -> none  [the longest x1 5.92 us: step(): wide = wide.sum(0).reshape(2, layers, rows, n, 2, n, deep)]
    convert_element_type x2 -> x1, other arithmetic: 10.7 us -> 4.98 us  [adamw(): return ((w - 0.02 * step).astype(BF16), m, v)]
where the time goes in v2:
time: 394 us
  Pallas kernels  388 us (98%)
  other arithmetic  4.98 us (1%)
    pallas_call x1, Pallas kernels, partial_sums(): pl.pallas_call(make_kernel(n, tokens, dim, rows, cols, deep, layers), out...  377 us
    pallas_call x1, Pallas kernels, step(): pl.pallas_call(gated_adamw(n, deep), grid=(layers, rows // tall), out_sha...  11 us

profile of v2, /device:TPU:97, one launch (start us, length us, event | category | flops | bytes accessed | tf_op | source)
XLA Modules:
  0.0 393.8 jit_solution(13271525499808717475)
XLA Ops:
  0.7 377.0 %shard_map.178 = (bf16[2,2,2,32,8192]{4,3,2,1,0:T(8,128)(2,1)}, f32[2,2,32,8192]{3,2,1,0:T(8,128)}, bf16[2,512,512]{2,1,0:T(8,128)(2,1)}, f32[2,512,512]{2,1,0:T(8,128)}) custom-call(bf16[1,1024,512]{2,1,0:T(8,128)(2,1)} %x_ref.1, bf16[1,1024,512]{2,1,0:T(8,128)(2,1)} %dy_ref.1, bf16[2,32,8192]{2,1,0:T(8,128)(2,1)} %wg.1, bf16[2,32,8192]{2,1,0:T(8,128)(2,1)} %wu.1, ...), custom_call_target="tpu_custom_call" | custom-call | tf_op jit(solution)/shard_map/pallas_call | solution.py:691
  377.7 0.0 copy-start
  377.7 0.0 copy-start.1
  377.7 11.0 %shard_map.179 = (bf16[2,32,8192]{2,1,0:T(8,128)(2,1)}, bf16[2,32,8192]{2,1,0:T(8,128)(2,1)}, f32[2,32,8192]{2,1,0:T(8,128)}, f32[2,32,8192]{2,1,0:T(8,128)}, f3...) custom-call(s32[1]{0:T(128)} %bitcast.near_ref, bf16[2,2,2,32,8192]{4,3,2,1,0:T(8,128)(2,1)} %get-tuple-element.19.far_ref, ...), custom_call_target="tpu_custom_call" | custom-call | tf_op jit(solution)/shard_map/pallas_call | solution.py:717
  388.8 0.0 copy-done
  388.8 0.0 copy-done.1
  388.8 5.0 %fusion.2 = (bf16[2,512,512]{2,1,0:T(8,128)(2,1)}, f32[2,512,512]{2,1,0:T(8,128)}, f32[2,512,512]{2,1,0:T(8,128)}) fusion(bf16[2,512,512]{2,1,0:T(8,128)(2,1)S(1)} %copy-done, f32[2,512,512]{2,1,0:T(8,128)S(1)} %copy-done.1, f32[2,512,512]{2,1,0:T(8,128)} %param.18, f32[2,512,512]{2,1,0:T(8,128)} %get-tuple-element.23, ...), kind=kLoop, calls=%fused_computation.6 | loop fusion | flops 9437184 | bytes 13631489 | tf_op jit(solution)/shard_map/convert_element_type | solution.py:20
Async XLA Ops:
  377.7 11.1 %copy-start = (bf16[2,512,512]{2,1,0:T(8,128)(2,1)S(1)}, bf16[2,512,512]{2,1,0:T(8,128)(2,1)}, u32[]{:S(2)}) copy-start(bf16[2,512,512]{2,1,0:T(8,128)(2,1)} %wd_ref.1) | copy-start | bytes 3145732
  377.7 11.1 %copy-start.1 = (f32[2,512,512]{2,1,0:T(8,128)S(1)}, f32[2,512,512]{2,1,0:T(8,128)}, u32[]{:S(2)}) copy-start(f32[2,512,512]{2,1,0:T(8,128)} %param.21) | copy-start | bytes 6291460
